TPU v7x, 128 devices: a whole 4x4x4 slice. The times are simulated.
128 devices in a mesh: dp: 8 (over z, core), mp: 16 (over y, x).
Axes of the slice: x: 4, y: 4, z: 4, core: 2. Of those that a mesh axis runs over, the one named last changes fastest.
Arguments:
- crop_hidden: bfloat16 [8, 1536, 8192], P(None, 'dp', 'mp'), may hold values from -15 to 15
- projector_weight: bfloat16 [8192, 8192], P('mp'), may hold values from -0.21213203 to 0.21213203
- pairing: int32 [8, 1536], P(None, 'dp'), may hold values from 0 to 191, as said below
Outputs:
- embeddings: float32 [8192, 8, 1536], P('mp', 'dp')
- loss_terms: float32 [4], replicated
Inputs may be any that keep to these rules, and one draw needn't show every extreme that they name: Each aligned block of 192 entries of a row of pairing is a permutation of 0 to 191.
All inputs are finite; a program needn't handle non-finite values.
Results may differ from a plain program's by a relative error of at most 0.0003.
Values may be sent and summed in bfloat16 or wider, within the bound.
No kernel may reach another device: no remote copies, remote signals or barrier semaphores. Data moves between devices by JAX's collectives and lax.ppermute only.
A program may use at most 128 MiB of HBM per device.

v0:
```python
import functools
import jax
import jax.numpy as jnp
from jax import lax
from jax.sharding import Mesh
from jax.sharding import PartitionSpec as P

MP = ("mp_0", "mp_1")
DP = ("dp_0", "dp_1")
DP_MP = ("dp_0", "dp_1", "mp_0", "mp_1")
highest = lax.Precision.HIGHEST
epsilon = 0.0001


def by_axis(x, axes):
    return functools.reduce(lax.psum, axes, x)


def local(crop_hidden, projector_weight, pairing):
    crop_count, local_rows, width_part = crop_hidden.shape
    features = projector_weight.shape[1]
    total_rows = crop_count * local_rows
    column_block = lax.all_to_all(projector_weight, MP, split_axis=1, concat_axis=0, tiled=True)
    shards = lax.all_gather(crop_hidden, MP, axis=2, tiled=True)
    flat_piece = shards.reshape(total_rows, shards.shape[2])
    embedded = lax.dot_general(
        column_block, flat_piece, (((0,), (1,)), ((), ())), preferred_element_type=jnp.float32
    )
    feature_part = embedded.shape[0]
    by_crop = embedded.reshape(feature_part, crop_count, local_rows)
    onehot = (pairing[:, :, None] == jnp.arange(local_rows, dtype=jnp.int32)[None, None, :]).astype(
        jnp.float32
    )
    aligned = jnp.einsum("jcr,cri->jci", by_crop, onehot, precision=highest)
    invariance = 0.0
    for anchor in range(2):
        differ = aligned - aligned[:, anchor : anchor + 1, :]
        invariance = invariance + jnp.sum(differ * differ)
    owned_block = lax.all_to_all(by_crop, DP, split_axis=1, concat_axis=2, tiled=True)
    batch_rows = owned_block.shape[2]
    column_mean = jnp.mean(owned_block, axis=2, keepdims=True)
    centered = owned_block - column_mean
    variance = jnp.sum(centered * centered, axis=2) / (batch_rows - 1)
    hinge_sum = jnp.sum(jax.nn.relu(1.0 - jnp.sqrt(variance + epsilon)))
    diagonal_sq = jnp.sum(variance * variance)
    gram_scale = 1.0 / ((batch_rows - 1) * (batch_rows - 1))
    partial_gram = jnp.einsum("jcr,jcs->crs", centered, centered, precision=highest)
    gram_block = lax.psum(partial_gram.astype(jnp.bfloat16), MP).astype(jnp.float32)
    frobenius = jnp.where(
        lax.axis_index(MP) == 0, jnp.sum(gram_block * gram_block) * gram_scale, 0.0
    )
    totals = (
        by_axis(invariance, DP_MP),
        by_axis(hinge_sum, DP_MP),
        by_axis(frobenius - diagonal_sq, DP_MP),
    )
    invariance_loss = totals[0] / (2 * (crop_count - 1) * batch_rows * features)
    variance_loss = totals[1] / (crop_count * features)
    covariance_loss = totals[2] / (crop_count * features)
    total_loss = 25.0 * invariance_loss + 25.0 * variance_loss + covariance_loss
    loss_terms = jnp.stack([invariance_loss, variance_loss, covariance_loss, total_loss])
    return (owned_block, loss_terms)


def solution(mesh):
    torus = Mesh(mesh.devices.reshape(4, 2, 4, 4), ("dp_0", "dp_1", "mp_0", "mp_1"))
    placed = (P(None, DP, MP), P(MP, None), P(None, DP))
    return jax.shard_map(
        local, mesh=torus, in_specs=placed, out_specs=(P(MP, DP, None), P()), check_vma=False
    )
```

profile of v0, /device:TPU:0, one launch (start us, length us, event | category | flops | bytes accessed | tf_op | source)
XLA Modules:
  0.0 498.9 jit_solution(17605152332946094416)
XLA Ops:
  7.2 0.0 all-gather.2.cloned.1.call-start
  7.2 0.7 all-gather.2.cloned.1.call-update
  7.9 0.0 all-reduce.6.cloned.1.call-start
  7.9 7.5 %copy.9 = bf16[64,16,8,512]{3,2,0,1:T(8,128)(2,1)} copy(bf16[64,16,8,512]{3,2,1,0:T(8,128)(2,1)} %bitcast.30) | data formatting | bytes 16777216 | tf_op jit(solution)/shard_map/all_to_all | solution.py:23
  15.4 128.3 %all_to_all.31 = bf16[512,16,512]{2,0,1:T(8,128)(2,1)} all-to-all(bf16[512,16,512]{2,0,1:T(8,128)(2,1)} %bitcast.29), channel_id=1, replica_groups=mesh['dp_0'=4,'dp_1'=2,'mp_0'=4,'mp_1'=4] {'mp_0','mp_1'}, dimensions={1} | all-to-all | bytes 16777216 | tf_op jit(solution)/shard_map/all_to_all | solution.py:23
  143.8 117.0 %all-gather.2.cloned.1.call-done = bf16[8,192,8192]{2,1,0:T(8,128)(2,1)} async-done(((bf16[8,192,512]{2,1,0:T(8,128)(2,1)}), bf16[8,192,8192]{2,1,0:T(8,128)(2,1)}) %all-gather.2.cloned.1.call-update) | async-done | bytes 25165840 | tf_op jit(solution)/shard_map/all_gather | solution.py:24
  260.8 18.9 %fusion.2 = f32[512,8,192]{0,2,1:T(8,128)S(1)} fusion(bf16[8192,512,1]{1,0,2:T(8,128)(2,1)} %bitcast.31, bf16[8,192,8192]{2,1,0:T(8,128)(2,1)} %all-gather.2.cloned.1.call-done), kind=kOutput, calls=%fused_computation.17 | convolution fusion | flops 12884901888 | bytes 36700160 | tf_op jit(solution)/shard_map/dot_general | solution.py:26
  279.7 0.0 copy-start
  279.7 1.7 copy-done
  281.3 42.7 %all_to_all.32 = f32[512,8,192]{0,2,1:T(8,128)S(1)} all-to-all(f32[512,8,192]{0,2,1:T(8,128)S(1)} %fusion.2), channel_id=1, replica_groups=mesh['dp_0'=4,'dp_1'=2,'mp_0'=4,'mp_1'=4] {'dp_0','dp_1'}, dimensions={1} | all-to-all | bytes 6291456 | tf_op jit(solution)/shard_map/all_to_all | solution.py:39
  324.0 0.3 reduce_sum.65
  324.3 0.6 multiply_reduce_fusion.1
  324.8 16.8 %fusion = bf16[1,1536,1536]{2,1,0:T(8,128)(2,1)} fusion(f32[512,1536]{0,1:T(8,128)S(1)} %bitcast.32), kind=kOutput, calls=%fused_computation.3 | convolution fusion | flops 14497873920 | bytes 7864320 | tf_op jit(solution)/shard_map/jcr,jcs->crs/dot_general | solution.py:47
  341.6 0.0 copy-start.1
  341.6 0.0 all-reduce.6.cloned.1.call-update
  341.6 0.7 copy-done.1
  342.3 3.9 convolution_bitcast_fusion
  346.2 0.1 slice_bitcast_fusion.1
  346.2 2.0 multiply_reduce_fusion.2
  349.5 5.4 %copy.6 = f32[512,1,1536]{2,1,0:T(1,128)} copy(f32[512,1,1536]{0,2,1:T(8,128)S(1)} %bitcast.28) | data formatting | bytes 6291456
  354.9 0.7 multiply_reduce_fusion.4
  355.6 91.4 %all-reduce.6.cloned.1.call-done = bf16[1,1536,1536]{2,1,0:T(8,128)(2,1)} async-done(((bf16[1,1536,1536]{2,1,0:T(8,128)(2,1)}), bf16[1,1536,1536]{2,1,0:T(8,128)(2,1)}) %all-reduce.6.cloned.1.call-update) | async-done | bytes 4718608 | tf_op jit(solution)/shard_map/psum | solution.py:48
  447.0 5.3 %multiply_reduce_fusion = f32[]{:T(128)} fusion(bf16[1,1536,1536]{2,1,0:T(8,128)(2,1)} %all-reduce.6.cloned.1.call-done), kind=kLoop, calls=%fused_computation | loop fusion | flops 7077887 | bytes 4718596 | tf_op jit(solution)/shard_map/reduce_sum | solution.py:50
  453.5 11.3 %all-reduce.2 = (f32[]{:T(128)}, f32[]{:T(128)}, f32[]{:T(128)}) all-reduce(f32[]{:T(128)S(6)} %add.47, f32[]{:T(128)} %get-tuple-element.7, f32[]{:T(128)S(6)} %sub.61), channel_id=1, replica_groups=mesh['dp_0'=4,'dp_1'=2,'mp_0'=4,'mp_1'=4] {'dp_0'}, use_global_device_ids=true, to_apply=%region_2.0 | all-reduce | flops 3 | bytes 24 | tf_op jit(solution)/shard_map/psum | solution.py:16
  464.8 3.2 all-reduce.3
  467.9 11.0 %all-reduce.1 = (f32[]{:T(128)}, f32[]{:T(128)}, f32[]{:T(128)}) all-reduce(f32[]{:T(128)} %get-tuple-element.17, f32[]{:T(128)} %get-tuple-element.18, f32[]{:T(128)} %get-tuple-element.19), channel_id=1, replica_groups=mesh['dp_0'=4,'dp_1'=2,'mp_0'=4,'mp_1'=4] {'mp_0'}, use_global_device_ids=true, to_apply=%region_4.5 | all-reduce | flops 3 | bytes 24 | tf_op jit(solution)/shard_map/psum | solution.py:16
  478.9 9.4 %all-reduce = (f32[]{:T(128)}, f32[]{:T(128)}, f32[]{:T(128)}) all-reduce(f32[]{:T(128)} %get-tuple-element.11, f32[]{:T(128)} %get-tuple-element.12, f32[]{:T(128)} %get-tuple-element.13), channel_id=1, replica_groups=mesh['dp_0'=4,'dp_1'=2,'mp_0'=4,'mp_1'=4] {'mp_1'}, use_global_device_ids=true, to_apply=%region_5.6 | all-reduce | flops 3 | bytes 24 | tf_op jit(solution)/shard_map/psum | solution.py:16
  491.5 0.6 pad_maximum_fusion
  (1 shorter events, 0.0 us)
Async XLA Ops:
  7.2 253.6 %all-gather.2.cloned.1.call-start = ((), (), s32[]{:S(2)}) async-start(), calls=%async_computation.2 | async-start | bytes 26738688 | tf_op jit(solution)/shard_map/all_gather | solution.py:24
  7.9 439.1 %all-reduce.6.cloned.1.call-start = ((), (), s32[]{:S(2)}) async-start(), calls=%async_computation.3 | async-start | bytes 9437184 | tf_op jit(solution)/shard_map/psum | solution.py:48
  279.7 1.7 copy-start
  341.6 0.7 copy-start.1
Sparse Core Ops, SparseCore 0:
  10.1 250.6 all-gather.1
  341.7 105.2 all-reduce.5
where the time goes:
time: 499 us
  waiting for transfers between devices  209 us (42%)
  blocking collectives  206 us (41%)
  matrix products  39.5 us (8%)
  between operations  19.8 us (4%)
  local copies, waits for them, and re-layouts  15.3 us (3%)
  other arithmetic  9.4 us (2%)
    all_to_all x1, blocking collectives, local(): lax.all_to_all(projector_weight, MP, split_axis=1, concat_axis=0, tiled=T...  128 us
    all_gather x1, waiting for transfers between devices, local(): shards = lax.all_gather(crop_hidden, MP, axis=2, tiled=True)  117 us
    psum x1, waiting for transfers between devices, local(): lax.psum(partial_gram.astype(jnp.bfloat16), MP).astype(jnp.float32)  91.4 us
    all_to_all x1, blocking collectives, local(): lax.all_to_all(by_crop, DP, split_axis=1, concat_axis=2, tiled=True)  42.7 us
    psum x4, blocking collectives, by_axis(): return functools.reduce(lax.psum, axes, x)  34.8 us
    dot_general x1, matrix products, local(): lax.dot_general(column_block, flat_piece, (((0,), (1,)), ((), ())), prefe...  18.9 us
    dot_general x1, matrix products, local(): jnp.einsum('jcr,jcs->crs', centered, centered, precision=highest)  16.8 us
  transfers between devices with their start and end apart: 2, of which 2 were waited for; matrix products, arithmetic and copies ran while one was open for 4% of the time, Pallas kernels for 0%

commit v1 on v0

--- a/solution.py
+++ b/solution.py
@@ -45,7 +45,12 @@
     diagonal_sq = jnp.sum(variance * variance)
     gram_scale = 1.0 / ((batch_rows - 1) * (batch_rows - 1))
     partial_gram = jnp.einsum("jcr,jcs->crs", centered, centered, precision=highest)
-    gram_block = lax.psum(partial_gram.astype(jnp.bfloat16), MP).astype(jnp.float32)
+
+    def fix_copies(work_x, dev_axis, axis_id="mp_1"):
+        item_now = jax.lax.psum(work_x, dev_axis)
+        return jax.lax.psum(item_now, axis_id)
+
+    gram_block = fix_copies(partial_gram.astype(jnp.bfloat16), "mp_0").astype(jnp.float32)
     frobenius = jnp.where(
         lax.axis_index(MP) == 0, jnp.sum(gram_block * gram_block) * gram_scale, 0.0
     )

time: 499 us -> 596 us (1.19)
  waiting for transfers between devices: 209 us -> 306 us
    psum x1 -> x2, waiting for transfers between devices: 91.4 us -> 189 us  [the longest x1 98.6 us: fix_copies(): item_now = jax.lax.psum(work_x, dev_axis)]
  transfers between devices with their start and end apart: 2 -> 3, of which waited for: 2 -> 3; matrix products, arithmetic and copies ran while one was open for 4% -> 3% of each run, Pallas kernels for 0% -> 0%
where the time goes in v1:
time: 596 us
  waiting for transfers between devices  306 us (51%)
  blocking collectives  206 us (35%)
  matrix products  39.5 us (7%)
  between operations  19.7 us (3%)
  local copies, waits for them, and re-layouts  14.6 us (2%)
  other arithmetic  9.51 us (2%)
    all_to_all x1, blocking collectives, local(): lax.all_to_all(projector_weight, MP, split_axis=1, concat_axis=0, tiled=T...  128 us
    all_gather x1, waiting for transfers between devices, local(): shards = lax.all_gather(crop_hidden, MP, axis=2, tiled=True)  117 us
    psum x1, waiting for transfers between devices, fix_copies(): item_now = jax.lax.psum(work_x, dev_axis)  98.6 us
    psum x1, waiting for transfers between devices, fix_copies(): return jax.lax.psum(item_now, axis_id)  90.1 us
    all_to_all x1, blocking collectives, local(): lax.all_to_all(by_crop, DP, split_axis=1, concat_axis=2, tiled=True)  42.7 us
    psum x4, blocking collectives, by_axis(): return functools.reduce(lax.psum, axes, x)  34.8 us
    dot_general x1, matrix products, local(): lax.dot_general(column_block, flat_piece, (((0,), (1,)), ((), ())), prefe...  18.9 us
    dot_general x1, matrix products, local(): jnp.einsum('jcr,jcs->crs', centered, centered, precision=highest)  16.8 us
  transfers between devices with their start and end apart: 3, of which 3 were waited for; matrix products, arithmetic and copies ran while one was open for 3% of the time, Pallas kernels for 0%

profile of v1, /device:TPU:0, one launch (start us, length us, event | category | flops | bytes accessed | tf_op | source)
XLA Modules:
  0.0 595.9 jit_solution(11724488774731935560)
XLA Ops:
  7.2 0.0 all-gather.2.cloned.1.call-start
  7.2 0.7 all-gather.2.cloned.1.call-update
  7.9 0.0 all-reduce.7.cloned.1.call-start
  7.9 7.5 %copy.9 = bf16[64,16,8,512]{3,2,0,1:T(8,128)(2,1)} copy(bf16[64,16,8,512]{3,2,1,0:T(8,128)(2,1)} %bitcast.30) | data formatting | bytes 16777216 | tf_op jit(solution)/shard_map/all_to_all | solution.py:23
  15.4 128.3 %all_to_all.31 = bf16[512,16,512]{2,0,1:T(8,128)(2,1)} all-to-all(bf16[512,16,512]{2,0,1:T(8,128)(2,1)} %bitcast.29), channel_id=1, replica_groups=mesh['dp_0'=4,'dp_1'=2,'mp_0'=4,'mp_1'=4] {'mp_0','mp_1'}, dimensions={1} | all-to-all | bytes 16777216 | tf_op jit(solution)/shard_map/all_to_all | solution.py:23
  143.8 117.0 %all-gather.2.cloned.1.call-done = bf16[8,192,8192]{2,1,0:T(8,128)(2,1)} async-done(((bf16[8,192,512]{2,1,0:T(8,128)(2,1)}), bf16[8,192,8192]{2,1,0:T(8,128)(2,1)}) %all-gather.2.cloned.1.call-update) | async-done | bytes 25165840 | tf_op jit(solution)/shard_map/all_gather | solution.py:24
  260.8 18.9 %fusion.2 = f32[512,8,192]{0,2,1:T(8,128)S(1)} fusion(bf16[8192,512,1]{1,0,2:T(8,128)(2,1)} %bitcast.31, bf16[8,192,8192]{2,1,0:T(8,128)(2,1)} %all-gather.2.cloned.1.call-done), kind=kOutput, calls=%fused_computation.17 | convolution fusion | flops 12884901888 | bytes 36700160 | tf_op jit(solution)/shard_map/dot_general | solution.py:26
  279.7 0.0 copy-start
  279.7 1.7 copy-done
  281.3 42.7 %all_to_all.32 = f32[512,8,192]{0,2,1:T(8,128)S(1)} all-to-all(f32[512,8,192]{0,2,1:T(8,128)S(1)} %fusion.2), channel_id=1, replica_groups=mesh['dp_0'=4,'dp_1'=2,'mp_0'=4,'mp_1'=4] {'dp_0','dp_1'}, dimensions={1} | all-to-all | bytes 6291456 | tf_op jit(solution)/shard_map/all_to_all | solution.py:39
  324.0 0.3 reduce_sum.65
  324.3 0.6 multiply_reduce_fusion.1
  324.8 16.8 %fusion = bf16[1,1536,1536]{2,1,0:T(8,128)(2,1)} fusion(f32[512,1536]{0,1:T(8,128)S(1)} %bitcast.32), kind=kOutput, calls=%fused_computation.3 | convolution fusion | flops 14497873920 | bytes 7864320 | tf_op jit(solution)/shard_map/jcr,jcs->crs/dot_general | solution.py:47
  341.6 0.0 all-reduce.7.cloned.1.call-update
  341.6 0.0 copy-start.1
  341.6 0.2 all-reduce.9.cloned.1.call-start
  341.8 98.6 %all-reduce.7.cloned.1.call-done = bf16[1,1536,1536]{2,1,0:T(8,128)(2,1)} async-done(((bf16[1,1536,1536]{2,1,0:T(8,128)(2,1)}), bf16[1,1536,1536]{2,1,0:T(8,128)(2,1)}) %all-reduce.7.cloned.1.call-update) | async-done | bytes 4718608 | tf_op jit(solution)/shard_map/psum | solution.py:50
  440.5 0.0 all-reduce.9.cloned.1.call-update
  440.5 0.0 copy-done.1
  440.5 3.9 convolution_bitcast_fusion
  444.4 0.1 slice_bitcast_fusion.1
  444.5 2.0 multiply_reduce_fusion.2
  447.8 5.4 copy.6
  453.2 0.7 multiply_reduce_fusion.4
  453.8 90.1 %all-reduce.9.cloned.1.call-done = bf16[1,1536,1536]{2,1,0:T(8,128)(2,1)} async-done(((bf16[1,1536,1536]{2,1,0:T(8,128)(2,1)}), bf16[1,1536,1536]{2,1,0:T(8,128)(2,1)}) %all-reduce.9.cloned.1.call-update) | async-done | bytes 4718608 | tf_op jit(solution)/shard_map/psum | solution.py:51
  544.0 5.4 multiply_reduce_fusion
  550.8 11.3 %all-reduce.2 = (f32[]{:T(128)}, f32[]{:T(128)}, f32[]{:T(128)}) all-reduce(f32[]{:T(128)S(6)} %add.49, f32[]{:T(128)} %get-tuple-element.7, f32[]{:T(128)S(6)} %sub.61), channel_id=1, replica_groups=mesh['dp_0'=4,'dp_1'=2,'mp_0'=4,'mp_1'=4] {'dp_0'}, use_global_device_ids=true, to_apply=%region_2.0 | all-reduce | flops 3 | bytes 24 | tf_op jit(solution)/shard_map/psum | solution.py:16
  562.0 3.2 all-reduce.3
  565.2 11.1 %all-reduce.1 = (f32[]{:T(128)}, f32[]{:T(128)}, f32[]{:T(128)}) all-reduce(f32[]{:T(128)} %get-tuple-element.17, f32[]{:T(128)} %get-tuple-element.18, f32[]{:T(128)} %get-tuple-element.19), channel_id=1, replica_groups=mesh['dp_0'=4,'dp_1'=2,'mp_0'=4,'mp_1'=4] {'mp_0'}, use_global_device_ids=true, to_apply=%region_4.5 | all-reduce | flops 3 | bytes 24 | tf_op jit(solution)/shard_map/psum | solution.py:16
  576.3 9.3 %all-reduce = (f32[]{:T(128)}, f32[]{:T(128)}, f32[]{:T(128)}) all-reduce(f32[]{:T(128)} %get-tuple-element.11, f32[]{:T(128)} %get-tuple-element.12, f32[]{:T(128)} %get-tuple-element.13), channel_id=1, replica_groups=mesh['dp_0'=4,'dp_1'=2,'mp_0'=4,'mp_1'=4] {'mp_1'}, use_global_device_ids=true, to_apply=%region_5.6 | all-reduce | flops 3 | bytes 24 | tf_op jit(solution)/shard_map/psum | solution.py:16
  588.8 0.6 pad_maximum_fusion
  (1 shorter events, 0.0 us)
Async XLA Ops:
  7.2 253.6 %all-gather.2.cloned.1.call-start = ((), (), s32[]{:S(2)}) async-start(), calls=%async_computation.2 | async-start | bytes 26738688 | tf_op jit(solution)/shard_map/all_gather | solution.py:24
  7.9 432.6 %all-reduce.7.cloned.1.call-start = ((), (), s32[]{:S(2)}) async-start(), calls=%async_computation.3 | async-start | bytes 9437184 | tf_op jit(solution)/shard_map/psum | solution.py:50
  279.7 1.7 copy-start
  341.6 98.9 %copy-start.1 = (s32[8,192]{1,0:T(8,128)S(1)}, s32[8,192]{1,0:T(8,128)}, u32[]{:S(2)}) copy-start(s32[8,192]{1,0:T(8,128)} %param.5) | copy-start | bytes 18436
  341.6 202.4 %all-reduce.9.cloned.1.call-start = ((), (), s32[]{:S(2)}) async-start(), calls=%async_computation.4 | async-start | bytes 9437184 | tf_op jit(solution)/shard_map/psum | solution.py:51
Sparse Core Ops, SparseCore 0:
  10.1 250.6 all-gather.1
  341.7 98.6 all-reduce.6
  442.8 101.0 all-reduce.8
